TPU v7x, 32 devices: a whole 2x2x4 slice. The times are simulated.
32 devices in a mesh: ep: 8 (over z, y), tp: 4 (over x, core).
Axes of the slice: x: 2, y: 2, z: 4, core: 2. Of those that a mesh axis runs over, the one named last changes fastest.
Arguments:
- tokens: bfloat16 [512, 4096], P(('ep', 'tp')), may hold values from -6 to 6
- routes: int32 [512, 2], P(('ep', 'tp')), may hold values from 0 to 7, all different within a row; in each aligned block of 16 rows (0 to 15, 16 to 31, ...) at most 8 rows name the same one
- combine: float32 [512, 2], P(('ep', 'tp')), may hold values from 0.25 to 1
- gate_weight: bfloat16 [8, 4096, 4096], P('ep', None, 'tp'), may hold values from -0.09375 to 0.09375
- up_weight: bfloat16 [8, 4096, 4096], P('ep', None, 'tp'), may hold values from -0.09375 to 0.09375
- down_weight: bfloat16 [8, 4096, 4096], P('ep', 'tp'), may hold values from -0.09375 to 0.09375
Outputs:
- moe_output: bfloat16 [512, 4096], P(('ep', 'tp'))
Inputs may be any that keep to these rules, and one draw needn't show every extreme that they name: `routes`: each row names 2 different experts. Among the rows of one device no expert is named more than 8 times, and in every draw some expert is named exactly 8 times by the rows of some device.
All inputs are finite; a program needn't handle non-finite values.
Results may differ from a plain program's by a relative error of at most 0.015.
Values may be sent and summed in bfloat16 or wider, within the bound.
A program may use at most 64 MiB of HBM per device.

v0:
```python
import jax
import jax.numpy as jnp
from jax import lax
from jax.sharding import PartitionSpec as P


def body(tokens, routes, combine, gate_weight, up_weight, down_weight):
    token_rows, feature_width = tokens.shape
    top_count = routes.shape[1]
    experts_here = gate_weight.shape[0]
    rank_count = lax.axis_size("ep")
    experts_all = experts_here * rank_count
    capacity = 2 * token_rows * top_count // experts_all
    flat_ids = routes.reshape(-1)
    onehot = (flat_ids[:, None] == jnp.arange(experts_all, dtype=jnp.int32)[None, :]).astype(
        jnp.int32
    )
    earlier = jnp.cumsum(onehot, axis=0) - onehot
    slot_index = jnp.sum(earlier * onehot, axis=1)
    target = flat_ids * capacity + slot_index
    selector = (
        target[:, None] == jnp.arange(experts_all * capacity, dtype=jnp.int32)[None, :]
    ).astype(jnp.bfloat16)
    repeated = jnp.repeat(tokens, top_count, axis=0)
    buffer = lax.dot_general(
        selector, repeated, (((0,), (0,)), ((), ())), preferred_element_type=jnp.float32
    ).astype(jnp.bfloat16)
    shaped = buffer.reshape(rank_count, 1, experts_here, capacity, feature_width)
    arrived = lax.all_to_all(shaped, "ep", split_axis=0, concat_axis=0, tiled=True)
    block_rows = lax.all_gather(arrived, "tp", axis=1, tiled=True)
    gate_values = jnp.einsum(
        "abecd,edf->abecf", block_rows, gate_weight, preferred_element_type=jnp.float32
    )
    up_values = jnp.einsum(
        "abecd,edf->abecf", block_rows, up_weight, preferred_element_type=jnp.float32
    )
    hidden = (jax.nn.silu(gate_values) * up_values).astype(jnp.bfloat16)
    partials = jnp.einsum(
        "abecf,efd->abecd", hidden, down_weight, preferred_element_type=jnp.float32
    )
    summed = lax.psum_scatter(partials.astype(jnp.bfloat16), "tp", scatter_dimension=1, tiled=True)
    returned = lax.all_to_all(summed, "ep", split_axis=0, concat_axis=0, tiled=True)
    returned = returned.reshape(experts_all * capacity, feature_width)
    picked = jnp.dot(selector, returned, preferred_element_type=jnp.float32).reshape(
        token_rows, top_count, feature_width
    )
    return jnp.sum(combine[:, :, None] * picked, axis=1).astype(jnp.bfloat16)


def solution(mesh):
    return jax.shard_map(
        body,
        mesh=mesh,
        in_specs=(
            P(("ep", "tp"), None),
            P(("ep", "tp"), None),
            P(("ep", "tp"), None),
            P("ep", None, "tp"),
            P("ep", None, "tp"),
            P("ep", "tp", None),
        ),
        out_specs=P(("ep", "tp"), None),
        check_vma=False,
    )
```

profile of v0, /device:TPU:0, one launch (start us, length us, event | category | flops | bytes accessed | tf_op | source)
XLA Modules:
  0.0 152.7 jit_solution(6297224300718134010)
XLA Ops:
  6.5 0.0 all-gather.2.cloned.1.call-start
  6.5 0.8 copy.24
  7.3 0.1 eq.50
  7.4 0.1 fusion.52
  7.5 0.1 reduce_window_sum.11
  7.5 0.2 select_reduce_fusion
  7.7 1.1 broadcast_in_dim.2
  8.8 0.1 reshape.65
  8.9 0.4 fusion.12
  9.3 21.7 %all_to_all.10 = bf16[8,1,1,8,4096]{4,3,1,2,0:T(8,128)(2,1)} all-to-all(bf16[8,1,1,8,4096]{4,3,1,2,0:T(8,128)(2,1)S(1)} %fusion.12), channel_id=1, replica_groups=mesh['ep'=8,'tp'=4] {'ep'}, dimensions={0} | all-to-all | bytes 1048576 | tf_op jit(solution)/shard_map/all_to_all | solution.py:29
  31.1 0.0 all-gather.2.cloned.1.call-update
  31.1 0.0 all-reduce.3.cloned.1.call-start
  31.2 21.7 %all-gather.2.cloned.1.call-done = bf16[8,4,1,8,4096]{4,3,1,0,2:T(8,128)(2,1)} async-done(((bf16[8,1,1,8,4096]{4,3,1,0,2:T(8,128)(2,1)}), bf16[8,4,1,8,4096]{4,3,1,0,2:T(8,128)(2,1)}) %all-gather.2.cloned.1.call-update) | async-done | bytes 2097168 | tf_op jit(solution)/shard_map/all_gather | solution.py:30
  52.8 0.0 copy-start.2
  52.8 6.5 %fusion.15 = f32[8,4,1,8,1024]{4,3,1,0,2:T(8,128)S(1)} fusion(bf16[1,4096,1024]{2,1,0:T(8,128)(2,1)} %param.9, bf16[8,4,1,8,4096]{4,3,1,0,2:T(8,128)(2,1)} %all-gather.2.cloned.1.call-done), kind=kOutput, calls=%fused_computation.13 | convolution fusion | flops 2147483648 | bytes 11534336 | tf_op jit(solution)/shard_map/abecd,edf->abecf/dot_general | solution.py:31
  59.3 0.0 copy-done.2
  59.3 0.0 copy-start.3
  59.4 0.0 copy-start
  59.4 0.0 copy-start.1
  59.4 11.7 %fusion.9 = bf16[8,4,1,8,4096]{4,3,1,0,2:T(8,128)(2,1)} fusion(bf16[1,1024,4096]{2,1,0:T(8,128)(2,1)} %param.11, bf16[1,4096,1024]{2,1,0:T(8,128)(2,1)} %param.10, bf16[8,4,1,8,4096]{4,3,1,0,2:T(8,128)(2,1)S(1)} %copy-done.2, f32[8,4,1,8,1024]{4,3,1,0,2:T(8,128)S(1)} %fusion.15), kind=kOutput, calls=%fused_computation.7 | convolution fusion | flops 4297588736 | bytes 22020096 | tf_op jit(solution)/shard_map/abecf,efd->abecd/dot_general | solution.py:38
  71.0 0.0 all-reduce.3.cloned.1.call-update
  71.1 0.0 copy-done.3
  71.1 0.6 dynamic-slice
  71.7 50.9 %all-reduce.3.cloned.1.call-done = bf16[8,4,1,8,4096]{4,3,1,0,2:T(8,128)(2,1)} async-done(((bf16[8,4,1,8,4096]{4,3,1,0,2:T(8,128)(2,1)}), bf16[8,4,1,8,4096]{4,3,1,0,2:T(8,128)(2,1)}) %all-reduce.3.cloned.1.call-update) | async-done | bytes 2097168
  122.6 2.5 %dynamic-slice_bitcast_fusion = bf16[8,1,1,8,4096]{4,3,1,2,0:T(8,128)(2,1)} fusion(bf16[8,4,1,8,4096]{4,3,1,0,2:T(8,128)(2,1)} %all-reduce.3.cloned.1.call-done, u32[]{:T(128)} %bitcast.44), kind=kLoop, calls=%fused_computation.25 | loop fusion | bytes 1048580 | tf_op jit(solution)/shard_map/reduce_scatter | solution.py:41
  125.1 5.5 %all-to-all-start.1 = ((bf16[8,1,1,8,4096]{4,3,1,2,0:T(8,128)(2,1)}), bf16[8,1,1,8,4096]{4,3,1,2,0:T(8,128)(2,1)S(1)}, u32[]{:S(2)}, u32[]{:S(2)}) async-start(bf16[8,1,1,8,4096]{4,3,1,2,0:T(8,128)(2,1)} %dynamic-slice_bitcast_fusion), calls=%async_computation.1 | async-start | bytes 1048576 | tf_op jit(solution)/shard_map/all_to_all | solution.py:42
  130.6 0.1 reduce_sum.21
  130.7 0.1 copy.25
  130.8 0.0 copy-done
  130.8 14.1 %all-to-all-done.1 = bf16[8,1,1,8,4096]{4,3,1,2,0:T(8,128)(2,1)S(1)} async-done(((bf16[8,1,1,8,4096]{4,3,1,2,0:T(8,128)(2,1)}), bf16[8,1,1,8,4096]{4,3,1,2,0:T(8,128)(2,1)S(1)}, u32[]{:S(2)}, u32[]{:S(2)}) %all-to-all-start.1) | async-done | bytes 524320 | tf_op jit(solution)/shard_map/all_to_all | solution.py:42
  144.9 0.0 copy-done.1
  144.9 0.9 fusion.44
  (2 shorter events, 0.0 us)
Async XLA Ops:
  6.5 46.3 %all-gather.2.cloned.1.call-start = ((), (), s32[]{:S(2)}) async-start(), calls=%async_computation.2 | async-start | bytes 2621440 | tf_op jit(solution)/shard_map/all_gather | solution.py:30
  31.1 91.5 %all-reduce.3.cloned.1.call-start = ((), (), s32[]{:S(2)}) async-start(), calls=%async_computation.3 | async-start | bytes 4194304
  52.8 6.5 %copy-start.2 = (bf16[8,4,1,8,4096]{4,3,1,0,2:T(8,128)(2,1)S(1)}, bf16[8,4,1,8,4096]{4,3,1,0,2:T(8,128)(2,1)}, u32[]{:S(2)}) copy-start(bf16[8,4,1,8,4096]{4,3,1,0,2:T(8,128)(2,1)} %all-gather.2.cloned.1.call-done) | copy-start | bytes 6291460
  59.3 11.7 %copy-start.3 = (u32[32]{0:T(128)S(1)}, u32[32]{0:T(128)}, u32[]{:S(2)}) copy-start(u32[32]{0:T(128)} %constant.21) | copy-start | bytes 388
  59.4 71.4 %copy-start = (s32[16,2]{0,1:T(2,128)S(1)}, s32[16,2]{0,1:T(2,128)}, u32[]{:S(2)}) copy-start(s32[16,2]{0,1:T(2,128)} %param.7) | copy-start | bytes 388
  59.4 85.5 %copy-start.1 = (f32[16,2]{0,1:T(2,128)S(1)}, f32[16,2]{0,1:T(2,128)}, u32[]{:S(2)}) copy-start(f32[16,2]{0,1:T(2,128)} %param.8) | copy-start | bytes 388
  125.1 19.8 %all-to-all-start.1 = ((bf16[8,1,1,8,4096]{4,3,1,2,0:T(8,128)(2,1)}), bf16[8,1,1,8,4096]{4,3,1,2,0:T(8,128)(2,1)S(1)}, u32[]{:S(2)}, u32[]{:S(2)}) async-start(bf16[8,1,1,8,4096]{4,3,1,2,0:T(8,128)(2,1)} %dynamic-slice_bitcast_fusion), calls=%async_computation.1 | async-start | bytes 1048576 | tf_op jit(solution)/shard_map/all_to_all | solution.py:42
Sparse Core Ops, SparseCore 0:
  31.2 21.5 all-gather.1
  71.2 51.3 all-reduce.2
where the time goes:
time: 153 us
  waiting for transfers between devices  86.7 us (57%)
  blocking collectives  21.7 us (14%)
  matrix products  19.5 us (13%)
  between operations  13.5 us (9%)
  starting transfers between devices  5.56 us (4%)
  local copies, waits for them, and re-layouts  5.33 us (3%)
    unnamed x3, waiting for transfers between devices  51 us
    all_to_all x1, blocking collectives, body(): lax.all_to_all(shaped, 'ep', split_axis=0, concat_axis=0, tiled=True)  21.7 us
    all_gather x1, waiting for transfers between devices, body(): block_rows = lax.all_gather(arrived, 'tp', axis=1, tiled=True)  21.7 us
    all_to_all x1, waiting for transfers between devices, body(): lax.all_to_all(summed, 'ep', split_axis=0, concat_axis=0, tiled=True)  14.1 us
    dot_general x1, matrix products, body(): jnp.einsum('abecf,efd->abecd', hidden, down_weight, preferred_element_typ...  11.7 us
    dot_general x1, matrix products, body(): jnp.einsum('abecd,edf->abecf', block_rows, gate_weight, preferred_element...  6.49 us
    all_to_all x1, starting transfers between devices, body(): lax.all_to_all(summed, 'ep', split_axis=0, concat_axis=0, tiled=True)  5.52 us
  transfers between devices with their start and end apart: 3, of which 3 were waited for; matrix products, arithmetic and copies ran while one was open for 0% of the time, Pallas kernels for 0%

commit v1 on v0

--- a/solution.py
+++ b/solution.py
@@ -27,7 +27,12 @@
     ).astype(jnp.bfloat16)
     shaped = buffer.reshape(rank_count, 1, experts_here, capacity, feature_width)
     arrived = lax.all_to_all(shaped, "ep", split_axis=0, concat_axis=0, tiled=True)
-    block_rows = lax.all_gather(arrived, "tp", axis=1, tiled=True)
+    ring = [arrived]
+    for hop in range(3):
+        ring.append(lax.ppermute(ring[-1], "tp", [(dev, (dev + 1) % 4) for dev in range(4)]))
+    block_rows = jnp.roll(
+        jnp.concatenate(ring[::-1], axis=1), (lax.axis_index("tp") + 1) * ring[0].shape[1], axis=1
+    )
     gate_values = jnp.einsum(
         "abecd,edf->abecf", block_rows, gate_weight, preferred_element_type=jnp.float32
     )

time: 153 us -> 158 us (1.033)
  waiting for transfers between devices: 86.7 us -> 89.9 us
  local copies, waits for them, and re-layouts: 5.33 us -> 7.54 us
    ppermute x0 -> x3, waiting for transfers between devices: none -> 25.8 us  [body(): lax.ppermute(ring[-1], 'tp', [(dev, (dev + 1) % 4) for dev in range(4)])]
    all_gather x1 -> x0, waiting for transfers between devices: 21.7 us -> none  [body(): block_rows = lax.all_gather(arrived, 'tp', axis=1, tiled=True)]
    unnamed x10 -> x17, local copies, waits for them, and re-layouts: 1.36 us -> 3.54 us
    unnamed x3 -> x2, waiting for transfers between devices: 51 us -> 50 us
  transfers between devices with their start and end apart: 3 -> 5, of which waited for: 3 -> 5; matrix products, arithmetic and copies ran while one was open for 0% -> 0% of each run, Pallas kernels for 0% -> 0%
where the time goes in v1:
time: 158 us
  waiting for transfers between devices  89.9 us (57%)
  blocking collectives  21.6 us (14%)
  matrix products  19.4 us (12%)
  between operations  13.5 us (9%)
  local copies, waits for them, and re-layouts  7.54 us (5%)
  starting transfers between devices  5.53 us (4%)
    unnamed x2, waiting for transfers between devices  50 us
    ppermute x3, waiting for transfers between devices, body(): lax.ppermute(ring[-1], 'tp', [(dev, (dev + 1) % 4) for dev in range(4)])  25.8 us
    all_to_all x1, blocking collectives, body(): lax.all_to_all(shaped, 'ep', split_axis=0, concat_axis=0, tiled=True)  21.6 us
    all_to_all x1, waiting for transfers between devices, body(): lax.all_to_all(summed, 'ep', split_axis=0, concat_axis=0, tiled=True)  14.1 us
    dot_general x1, matrix products, body(): jnp.einsum('abecf,efd->abecd', hidden, down_weight, preferred_element_typ...  12.3 us
    dot_general x1, matrix products, body(): jnp.einsum('abecd,edf->abecf', block_rows, gate_weight, preferred_element...  5.78 us
    all_to_all x1, starting transfers between devices, body(): lax.all_to_all(summed, 'ep', split_axis=0, concat_axis=0, tiled=True)  5.52 us
    unnamed x17, local copies, waits for them, and re-layouts  3.54 us
  transfers between devices with their start and end apart: 5, of which 5 were waited for; matrix products, arithmetic and copies ran while one was open for 0% of the time, Pallas kernels for 0%

profile of v1, /device:TPU:0, one launch (start us, length us, event | category | flops | bytes accessed | tf_op | source)
XLA Modules:
  0.0 157.8 jit_solution(14847909438469543599)
XLA Ops:
  6.5 0.0 all-reduce.3.cloned.1.call-start
  6.5 0.8 copy.23
  7.3 0.1 eq.53
  7.4 0.1 fusion.38
  7.5 0.1 reduce_window_sum.11
  7.5 0.2 select_reduce_fusion
  7.7 1.1 broadcast_in_dim.2
  8.8 0.1 reshape.65
  8.9 0.4 fusion.12
  9.3 21.6 %all_to_all.10 = bf16[8,1,1,8,4096]{4,3,2,1,0:T(8,128)(2,1)S(1)} all-to-all(bf16[8,1,1,8,4096]{4,3,2,1,0:T(8,128)(2,1)S(1)} %fusion.12), channel_id=1, replica_groups=mesh['ep'=8,'tp'=4] {'ep'}, dimensions={0} | all-to-all | bytes 1048576 | tf_op jit(solution)/shard_map/all_to_all | solution.py:29
  31.0 0.0 collective-permute-start
  31.0 8.6 %collective-permute-done = bf16[8,1,1,8,4096]{4,3,2,1,0:T(8,128)(2,1)S(1)} collective-permute-done((bf16[8,1,1,8,4096]{4,3,2,1,0:T(8,128)(2,1)S(1)}, bf16[8,1,1,8,4096]{4,3,2,1,0:T(8,128)(2,1)S(1)}, u32[]{:S(2)}, u32[]{:S(2)}) %collective-permute-start) | collective-permute-done | bytes 524320 | tf_op jit(solution)/shard_map/ppermute | solution.py:32
  39.6 0.0 collective-permute-start.1
  39.6 8.6 %collective-permute-done.1 = bf16[8,1,1,8,4096]{4,3,2,1,0:T(8,128)(2,1)S(1)} collective-permute-done((bf16[8,1,1,8,4096]{4,3,2,1,0:T(8,128)(2,1)S(1)}, bf16[8,1,1,8,4096]{4,3,2,1,0:T(8,128)(2,1)S(1)}, u32[]{:S(2)}, u32[]{:S(2)}) %collective-permute-start.1) | collective-permute-done | bytes 524320 | tf_op jit(solution)/shard_map/ppermute | solution.py:32
  48.2 0.0 collective-permute-start.2
  48.2 8.6 %collective-permute-done.2 = bf16[8,1,1,8,4096]{4,3,2,1,0:T(8,128)(2,1)S(1)} collective-permute-done((bf16[8,1,1,8,4096]{4,3,2,1,0:T(8,128)(2,1)S(1)}, bf16[8,1,1,8,4096]{4,3,2,1,0:T(8,128)(2,1)S(1)}, u32[]{:S(2)}, u32[]{:S(2)}) %collective-permute-start.2) | collective-permute-done | bytes 524320 | tf_op jit(solution)/shard_map/ppermute | solution.py:32
  57.2 0.0 copy-start
  57.2 1.9 %copy-done = bf16[8,8,1,8,4096]{4,3,2,1,0:T(8,128)(2,1)} copy-done((bf16[8,8,1,8,4096]{4,3,2,1,0:T(8,128)(2,1)}, bf16[8,8,1,8,4096]{4,3,2,1,0:T(8,128)(2,1)S(1)}, u32[]{:S(2)}) %copy-start) | copy-done | bytes 4194328
  59.1 5.8 %fusion.17 = f32[8,4,1,8,1024]{4,3,1,0,2:T(8,128)S(1)} fusion(bf16[1,4096,1024]{2,1,0:T(8,128)(2,1)} %param.9, bf16[8,8,1,8,4096]{4,3,2,1,0:T(8,128)(2,1)S(1)} %constant_dynamic-update-slice_fusion, s32[]{:T(128)S(6)} %select_n.14), kind=kOutput, calls=%fused_computation.15 | convolution fusion | flops 2147483648 | bytes 11534340 | tf_op jit(solution)/shard_map/abecd,edf->abecf/dot_general | solution.py:36
  64.9 0.0 copy-start.3
  64.9 12.3 %fusion.9 = bf16[8,4,1,8,4096]{4,3,1,0,2:T(8,128)(2,1)} fusion(bf16[1,1024,4096]{2,1,0:T(8,128)(2,1)} %param.11, f32[8,4,1,8,1024]{4,3,1,0,2:T(8,128)S(1)} %fusion.17, bf16[1,4096,1024]{2,1,0:T(8,128)(2,1)} %param.10, bf16[8,8,1,8,4096]{4,3,2,1,0:T(8,128)(2,1)} %copy-done, s32[]{:T(128)S(6)} %select_n.14), kind=kOutput, calls=%fused_computation.7 | convolution fusion | flops 4297588736 | bytes 22020100 | tf_op jit(solution)/shard_map/abecf,efd->abecd/dot_general | solution.py:43
  77.2 0.0 copy-start.1
  77.2 0.0 copy-start.2
  77.2 0.0 all-reduce.3.cloned.1.call-update
  77.2 0.0 copy-done.3
  77.2 0.6 dynamic-slice
  77.8 49.9 %all-reduce.3.cloned.1.call-done = bf16[8,4,1,8,4096]{4,3,1,0,2:T(8,128)(2,1)} async-done(((bf16[8,4,1,8,4096]{4,3,1,0,2:T(8,128)(2,1)}), bf16[8,4,1,8,4096]{4,3,1,0,2:T(8,128)(2,1)}) %all-reduce.3.cloned.1.call-update) | async-done | bytes 2097168
  127.7 2.5 %dynamic-slice_bitcast_fusion = bf16[8,1,1,8,4096]{4,3,1,2,0:T(8,128)(2,1)} fusion(bf16[8,4,1,8,4096]{4,3,1,0,2:T(8,128)(2,1)} %all-reduce.3.cloned.1.call-done, u32[]{:T(128)} %bitcast.43), kind=kLoop, calls=%fused_computation.20 | loop fusion | bytes 1048580 | tf_op jit(solution)/shard_map/reduce_scatter | solution.py:46
  130.2 5.5 %all-to-all-start.1 = ((bf16[8,1,1,8,4096]{4,3,1,2,0:T(8,128)(2,1)}), bf16[8,1,1,8,4096]{4,3,1,2,0:T(8,128)(2,1)S(1)}, u32[]{:S(2)}, u32[]{:S(2)}) async-start(bf16[8,1,1,8,4096]{4,3,1,2,0:T(8,128)(2,1)} %dynamic-slice_bitcast_fusion), calls=%async_computation.1 | async-start | bytes 1048576 | tf_op jit(solution)/shard_map/all_to_all | solution.py:47
  135.8 0.1 reduce_sum.21
  135.8 0.1 copy.24
  135.9 0.0 copy-done.1
  135.9 14.1 %all-to-all-done.1 = bf16[8,1,1,8,4096]{4,3,1,2,0:T(8,128)(2,1)S(1)} async-done(((bf16[8,1,1,8,4096]{4,3,1,2,0:T(8,128)(2,1)}), bf16[8,1,1,8,4096]{4,3,1,2,0:T(8,128)(2,1)S(1)}, u32[]{:S(2)}, u32[]{:S(2)}) %all-to-all-start.1) | async-done | bytes 524320 | tf_op jit(solution)/shard_map/all_to_all | solution.py:47
  150.0 0.0 copy-done.2
  150.0 0.9 fusion.27
  (10 shorter events, 0.3 us)
Async XLA Ops:
  6.5 121.2 %all-reduce.3.cloned.1.call-start = ((), (), s32[]{:S(2)}) async-start(), calls=%async_computation.2 | async-start | bytes 4194304
  31.0 8.6 %collective-permute-start = (bf16[8,1,1,8,4096]{4,3,2,1,0:T(8,128)(2,1)S(1)}, bf16[8,1,1,8,4096]{4,3,2,1,0:T(8,128)(2,1)S(1)}, u32[]{:S(2)}, u32[]{:S(2)}) collective-permute-start(bf16[8,1,1,8,4096]{4,3,2,1,0:T(8,128)(2,1)S(1)} %all_to_all.10), channel_id=1, source_target_pairs={{0,1},{1,2},{2,3},{3,0},{4,5},{5,6},{6,7},{7,4},{8,9},{9,10},{10,1... | collective-permute-start | bytes 1572872 | tf_op jit(solution)/shard_map/ppermute | solution.py:32
  39.6 8.6 %collective-permute-start.1 = (bf16[8,1,1,8,4096]{4,3,2,1,0:T(8,128)(2,1)S(1)}, bf16[8,1,1,8,4096]{4,3,2,1,0:T(8,128)(2,1)S(1)}, u32[]{:S(2)}, u32[]{:S(2)}) collective-permute-start(bf16[8,1,1,8,4096]{4,3,2,1,0:T(8,128)(2,1)S(1)} %collective-permute-done), channel_id=1, source_target_pairs={{0,1},{1,2},{2,3},{3,0},{4,5},{5,6},{6,7},{7,4},{8,9},{9,10},{10,1... | collective-permute-start | bytes 1572872 | tf_op jit(solution)/shard_map/ppermute | solution.py:32
  48.2 8.6 %collective-permute-start.2 = (bf16[8,1,1,8,4096]{4,3,2,1,0:T(8,128)(2,1)S(1)}, bf16[8,1,1,8,4096]{4,3,2,1,0:T(8,128)(2,1)S(1)}, u32[]{:S(2)}, u32[]{:S(2)}) collective-permute-start(bf16[8,1,1,8,4096]{4,3,2,1,0:T(8,128)(2,1)S(1)} %collective-permute-done.1), channel_id=1, source_target_pairs={{0,1},{1,2},{2,3},{3,0},{4,5},{5,6},{6,7},{7,4},{8,9},{9,10},{10,1... | collective-permute-start | bytes 1572872 | tf_op jit(solution)/shard_map/ppermute | solution.py:32
  57.2 1.9 %copy-start = (bf16[8,8,1,8,4096]{4,3,2,1,0:T(8,128)(2,1)}, bf16[8,8,1,8,4096]{4,3,2,1,0:T(8,128)(2,1)S(1)}, u32[]{:S(2)}) copy-start(bf16[8,8,1,8,4096]{4,3,2,1,0:T(8,128)(2,1)S(1)} %constant_dynamic-update-slice_fusion) | copy-start | bytes 12582916
  64.9 12.3 %copy-start.3 = (u32[32]{0:T(128)S(1)}, u32[32]{0:T(128)}, u32[]{:S(2)}) copy-start(u32[32]{0:T(128)} %constant.48) | copy-start | bytes 388
  77.2 58.8 %copy-start.1 = (s32[16,2]{0,1:T(2,128)S(1)}, s32[16,2]{0,1:T(2,128)}, u32[]{:S(2)}) copy-start(s32[16,2]{0,1:T(2,128)} %param.7) | copy-start | bytes 388
  77.2 72.9 %copy-start.2 = (f32[16,2]{0,1:T(2,128)S(1)}, f32[16,2]{0,1:T(2,128)}, u32[]{:S(2)}) copy-start(f32[16,2]{0,1:T(2,128)} %param.8) | copy-start | bytes 388
  130.2 19.8 %all-to-all-start.1 = ((bf16[8,1,1,8,4096]{4,3,1,2,0:T(8,128)(2,1)}), bf16[8,1,1,8,4096]{4,3,1,2,0:T(8,128)(2,1)S(1)}, u32[]{:S(2)}, u32[]{:S(2)}) async-start(bf16[8,1,1,8,4096]{4,3,1,2,0:T(8,128)(2,1)} %dynamic-slice_bitcast_fusion), calls=%async_computation.1 | async-start | bytes 1048576 | tf_op jit(solution)/shard_map/all_to_all | solution.py:47
Sparse Core Ops, SparseCore 0:
  77.3 50.3 all-reduce.2
